TPU v7x, 128 devices: a whole 4x4x4 slice. The times are simulated.
128 devices in a mesh: data: 1, time: 128 (over z, y, x, core).
Axes of the slice: x: 4, y: 4, z: 4, core: 2. Of those that a mesh axis runs over, the one named last changes fastest.
Arguments:
- x_init: float32 [4, 64, 768], P('data')
- w_in: bfloat16 [768, 3072], replicated
- w_out: bfloat16 [3072, 768], replicated
- mod_gamma: bfloat16 [1024, 3072], P('time')
- mod_beta: bfloat16 [1024, 3072], P('time')
- step_size: float32 [1024], P('time')
Outputs:
- output: float32 [4, 64, 768], P('data')
All inputs are finite; a program needn't handle non-finite values.
Results may differ from a plain program's by a relative error of at most 0.001.
Values are sent between devices in bfloat16 or wider.
A program may use at most 1 GiB of HBM per device.

v0:
```python
import jax
import jax.numpy as jnp
from jax import lax
from jax.sharding import PartitionSpec as P

SWEEPS = 4


def solution(mesh):
    groups = mesh.shape["time"]
    distances = [2 ** level for level in range(12) if 2 ** level < groups]

    def prefix_of(own_total):
        prefix = jnp.zeros_like(own_total)
        inclusive = own_total
        for distance in distances:
            send_pairs = [(source, source + distance) for source in range(groups - distance)]
            received = lax.ppermute(inclusive, "time", send_pairs)
            inclusive = inclusive + received
            prefix = prefix + received
        return prefix

    def local_run(x_init, w_in, w_out, mod_gamma, mod_beta, step_size):
        mod_scale = (1.0 + mod_gamma.astype(jnp.float32))[:, None, None, :]
        mod_shift = mod_beta.astype(jnp.float32)[:, None, None, :]
        h_steps = step_size[:, None, None, None]
        pre_act = jnp.einsum("bnc,cd->bnd", x_init.astype(jnp.bfloat16), w_in, preferred_element_type=jnp.float32)[None]
        result = x_init
        for sweep_idx in range(SWEEPS):
            hidden_act = jax.nn.gelu(pre_act * mod_scale + mod_shift, approximate=True).astype(jnp.bfloat16)
            drifts = jnp.einsum("kbnd,dc->kbnc", hidden_act, w_out, preferred_element_type=jnp.float32) * h_steps
            if sweep_idx < SWEEPS - 1:
                running = jnp.cumsum(drifts, axis=0)
                latents = x_init + prefix_of(running[-1]) + (running - drifts)
                pre_act = jnp.einsum("kbnc,cd->kbnd", latents.astype(jnp.bfloat16), w_in, preferred_element_type=jnp.float32)
            else:
                result = x_init + lax.psum(jnp.sum(drifts, axis=0), "time")
        return result

    return jax.shard_map(local_run, mesh=mesh, in_specs=(P("data", None, None), P(None, None), P(None, None), P("time", None), P("time", None), P("time")), out_specs=P("data", None, None), check_vma=False)
```

profile of v0, /device:TPU:1, one launch (start us, length us, event | category | flops | bytes accessed | tf_op | source)
XLA Modules:
  0.0 709.7 jit_solution(2874966456159774199)
XLA Ops:
  12.6 29.8 %fusion.32 = f32[8,4,64,768]{3,2,1,0:T(8,128)S(1)} fusion(f32[8,3072]{1,0:T(8,128)S(1)} %convert_element_type.32, f32[8,3072]{1,0:T(8,128)S(1)} %convert_add_fusion, f32[4,64,3072]{2,1,0:T(8,128)S(1)} %fusion.75, bf16[3072,768]{1,0:T(8,128)(2,1)S(1)} %bitcast.52), kind=kOutput, calls=%fused_computation.36 | convolution fusion | flops 9732882432 | bytes 14352384 | tf_op jit(solution)/shard_map/kbnd,dc->kbnc/dot_general | solution.py:31
  49.6 8.9 %collective-permute-done = f32[4,64,768]{2,1,0:T(8,128)S(1)} collective-permute-done((f32[4,64,768]{2,1,0:T(8,128)S(1)}, f32[4,64,768]{2,1,0:T(8,128)S(1)}, u32[]{:S(2)}, u32[]{:S(2)}) %collective-permute-start) | collective-permute-done | bytes 786464 | tf_op jit(solution)/shard_map/ppermute | solution.py:18
  62.0 15.4 %collective-permute-done.1 = f32[4,64,768]{2,1,0:T(8,128)S(1)} collective-permute-done((f32[4,64,768]{2,1,0:T(8,128)S(1)}, f32[4,64,768]{2,1,0:T(8,128)S(1)}, u32[]{:S(2)}, u32[]{:S(2)}) %collective-permute-start.1) | collective-permute-done | bytes 786464 | tf_op jit(solution)/shard_map/ppermute | solution.py:18
  82.6 14.3 %collective-permute-done.2 = f32[4,64,768]{2,1,0:T(8,128)S(1)} collective-permute-done((f32[4,64,768]{2,1,0:T(8,128)S(1)}, f32[4,64,768]{2,1,0:T(8,128)S(1)}, u32[]{:S(2)}, u32[]{:S(2)}) %collective-permute-start.2) | collective-permute-done | bytes 786464 | tf_op jit(solution)/shard_map/ppermute | solution.py:18
  100.6 11.3 %collective-permute-done.3 = f32[4,64,768]{2,1,0:T(8,128)S(1)} collective-permute-done((f32[4,64,768]{2,1,0:T(8,128)S(1)}, f32[4,64,768]{2,1,0:T(8,128)S(1)}, u32[]{:S(2)}, u32[]{:S(2)}) %collective-permute-start.3) | collective-permute-done | bytes 786464 | tf_op jit(solution)/shard_map/ppermute | solution.py:18
  117.8 8.9 %collective-permute-done.4 = f32[4,64,768]{2,1,0:T(8,128)S(1)} collective-permute-done((f32[4,64,768]{2,1,0:T(8,128)S(1)}, f32[4,64,768]{2,1,0:T(8,128)S(1)}, u32[]{:S(2)}, u32[]{:S(2)}) %collective-permute-start.4) | collective-permute-done | bytes 786464 | tf_op jit(solution)/shard_map/ppermute | solution.py:18
  133.0 17.3 %collective-permute-done.5 = f32[4,64,768]{2,1,0:T(8,128)S(1)} collective-permute-done((f32[4,64,768]{2,1,0:T(8,128)S(1)}, f32[4,64,768]{2,1,0:T(8,128)S(1)}, u32[]{:S(2)}, u32[]{:S(2)}) %collective-permute-start.5) | collective-permute-done | bytes 786464 | tf_op jit(solution)/shard_map/ppermute | solution.py:18
  156.3 13.4 %collective-permute-done.6 = f32[4,64,768]{2,1,0:T(8,128)S(1)} collective-permute-done((f32[4,64,768]{2,1,0:T(8,128)S(1)}, f32[4,64,768]{2,1,0:T(8,128)S(1)}, u32[]{:S(2)}, u32[]{:S(2)}) %collective-permute-start.6) | collective-permute-done | bytes 786464 | tf_op jit(solution)/shard_map/ppermute | solution.py:18
  170.0 28.5 %fusion.45 = f32[8,4,64,768]{3,2,1,0:T(8,128)} fusion(f32[8,3072]{1,0:T(8,128)S(1)} %convert_element_type.32, f32[8,3072]{1,0:T(8,128)S(1)} %convert_add_fusion, bf16[768,3072]{1,0:T(8,128)(2,1)} %param.7, bf16[3072,768]{1,0:T(8,128)(2,1)} %param.8, f32[8,4,64,768]{3,2,1,0:T(8,128)} %copy-done.2, f32[8,4,64,768]{3,2,1,0:T(8,128)} %copy-done.4, ...), kind=kOutput, calls=%fused_computation.46 | convolution fusion | flops 19402850304 | bytes 29294624 | tf_op jit(solution)/shard_map/kbnd,dc->kbnc/dot_general | solution.py:31
  202.2 14.5 %collective-permute-start.7 = (f32[4,64,768]{2,1,0:T(8,128)S(1)}, f32[4,64,768]{2,1,0:T(8,128)S(1)}, u32[]{:S(2)}, u32[]{:S(2)}) collective-permute-start(f32[4,64,768]{2,1,0:T(8,128)S(1)} %slice_bitcast_fusion.1), channel_id=1, source_target_pairs={{0,1},{1,2},{2,3},{3,4},{4,5},{5,6},{6,7},{7,8},{8,9},{9,10},{10,1... | collective-permute-start | bytes 2359304 | tf_op jit(solution)/shard_map/ppermute | solution.py:18
  216.7 8.9 %collective-permute-done.7 = f32[4,64,768]{2,1,0:T(8,128)S(1)} collective-permute-done((f32[4,64,768]{2,1,0:T(8,128)S(1)}, f32[4,64,768]{2,1,0:T(8,128)S(1)}, u32[]{:S(2)}, u32[]{:S(2)}) %collective-permute-start.7) | collective-permute-done | bytes 786464 | tf_op jit(solution)/shard_map/ppermute | solution.py:18
  227.5 14.0 %collective-permute-done.8 = f32[4,64,768]{2,1,0:T(8,128)S(1)} collective-permute-done((f32[4,64,768]{2,1,0:T(8,128)S(1)}, f32[4,64,768]{2,1,0:T(8,128)S(1)}, u32[]{:S(2)}, u32[]{:S(2)}) %collective-permute-start.8) | collective-permute-done | bytes 786464 | tf_op jit(solution)/shard_map/ppermute | solution.py:18
  241.5 10.6 %collective-permute-start.9 = (f32[4,64,768]{2,1,0:T(8,128)S(1)}, f32[4,64,768]{2,1,0:T(8,128)S(1)}, u32[]{:S(2)}, u32[]{:S(2)}) collective-permute-start(f32[4,64,768]{2,1,0:T(8,128)S(1)} %add.228), channel_id=1, source_target_pairs={{0,4},{1,5},{2,6},{3,7},{4,8},{5,9},{6,10},{7,11},{8,12},{9,13},{1... | collective-permute-start | bytes 2359304 | tf_op jit(solution)/shard_map/ppermute | solution.py:18
  252.1 16.8 %collective-permute-done.9 = f32[4,64,768]{2,1,0:T(8,128)S(1)} collective-permute-done((f32[4,64,768]{2,1,0:T(8,128)S(1)}, f32[4,64,768]{2,1,0:T(8,128)S(1)}, u32[]{:S(2)}, u32[]{:S(2)}) %collective-permute-start.9) | collective-permute-done | bytes 786464 | tf_op jit(solution)/shard_map/ppermute | solution.py:18
  270.4 12.8 %collective-permute-done.10 = f32[4,64,768]{2,1,0:T(8,128)S(1)} collective-permute-done((f32[4,64,768]{2,1,0:T(8,128)S(1)}, f32[4,64,768]{2,1,0:T(8,128)S(1)}, u32[]{:S(2)}, u32[]{:S(2)}) %collective-permute-start.10) | collective-permute-done | bytes 786464 | tf_op jit(solution)/shard_map/ppermute | solution.py:18
  288.5 12.4 %collective-permute-done.11 = f32[4,64,768]{2,1,0:T(8,128)S(1)} collective-permute-done((f32[4,64,768]{2,1,0:T(8,128)S(1)}, f32[4,64,768]{2,1,0:T(8,128)S(1)}, u32[]{:S(2)}, u32[]{:S(2)}) %collective-permute-start.11) | collective-permute-done | bytes 786464 | tf_op jit(solution)/shard_map/ppermute | solution.py:18
  306.9 12.9 %collective-permute-done.12 = f32[4,64,768]{2,1,0:T(8,128)S(1)} collective-permute-done((f32[4,64,768]{2,1,0:T(8,128)S(1)}, f32[4,64,768]{2,1,0:T(8,128)S(1)}, u32[]{:S(2)}, u32[]{:S(2)}) %collective-permute-start.12) | collective-permute-done | bytes 786464 | tf_op jit(solution)/shard_map/ppermute | solution.py:18
  320.0 10.0 %collective-permute-start.13 = (f32[4,64,768]{2,1,0:T(8,128)S(1)}, f32[4,64,768]{2,1,0:T(8,128)S(1)}, u32[]{:S(2)}, u32[]{:S(2)}) collective-permute-start(f32[4,64,768]{2,1,0:T(8,128)S(1)} %add.236), channel_id=1, source_target_pairs={{0,64},{1,65},{2,66},{3,67},{4,68},{5,69},{6,70},{7,71},{8,72},{9,... | collective-permute-start | bytes 2359304 | tf_op jit(solution)/shard_map/ppermute | solution.py:18
  330.0 8.5 %collective-permute-done.13 = f32[4,64,768]{2,1,0:T(8,128)S(1)} collective-permute-done((f32[4,64,768]{2,1,0:T(8,128)S(1)}, f32[4,64,768]{2,1,0:T(8,128)S(1)}, u32[]{:S(2)}, u32[]{:S(2)}) %collective-permute-start.13) | collective-permute-done | bytes 786464 | tf_op jit(solution)/shard_map/ppermute | solution.py:18
  338.8 28.4 %fusion.43 = f32[8,4,64,768]{3,2,1,0:T(8,128)} fusion(f32[8,3072]{1,0:T(8,128)S(1)} %convert_element_type.32, f32[8,3072]{1,0:T(8,128)S(1)} %convert_add_fusion, bf16[768,3072]{1,0:T(8,128)(2,1)} %param.7, bf16[3072,768]{1,0:T(8,128)(2,1)} %param.8, f32[8,4,64,768]{3,2,1,0:T(8,128)} %copy-done.3, f32[8,4,64,768]{3,2,1,0:T(8,128)} %fusion.45, ...), kind=kOutput, calls=%fused_computation.45 | convolution fusion | flops 19402850304 | bytes 29294624 | tf_op jit(solution)/shard_map/kbnd,dc->kbnc/dot_general | solution.py:31
  371.0 19.3 %collective-permute-start.14 = (f32[4,64,768]{2,1,0:T(8,128)S(1)}, f32[4,64,768]{2,1,0:T(8,128)S(1)}, u32[]{:S(2)}, u32[]{:S(2)}) collective-permute-start(f32[4,64,768]{2,1,0:T(8,128)S(1)} %slice_bitcast_fusion), channel_id=1, source_target_pairs={{0,1},{1,2},{2,3},{3,4},{4,5},{5,6},{6,7},{7,8},{8,9},{9,10},{10,1... | collective-permute-start | bytes 2359304 | tf_op jit(solution)/shard_map/ppermute | solution.py:18
  390.2 8.9 %collective-permute-done.14 = f32[4,64,768]{2,1,0:T(8,128)S(1)} collective-permute-done((f32[4,64,768]{2,1,0:T(8,128)S(1)}, f32[4,64,768]{2,1,0:T(8,128)S(1)}, u32[]{:S(2)}, u32[]{:S(2)}) %collective-permute-start.14) | collective-permute-done | bytes 786464 | tf_op jit(solution)/shard_map/ppermute | solution.py:18
  400.6 13.6 %collective-permute-done.15 = f32[4,64,768]{2,1,0:T(8,128)S(1)} collective-permute-done((f32[4,64,768]{2,1,0:T(8,128)S(1)}, f32[4,64,768]{2,1,0:T(8,128)S(1)}, u32[]{:S(2)}, u32[]{:S(2)}) %collective-permute-start.15) | collective-permute-done | bytes 786464 | tf_op jit(solution)/shard_map/ppermute | solution.py:18
  415.6 14.8 %collective-permute-done.16 = f32[4,64,768]{2,1,0:T(8,128)S(1)} collective-permute-done((f32[4,64,768]{2,1,0:T(8,128)S(1)}, f32[4,64,768]{2,1,0:T(8,128)S(1)}, u32[]{:S(2)}, u32[]{:S(2)}) %collective-permute-start.16) | collective-permute-done | bytes 786464 | tf_op jit(solution)/shard_map/ppermute | solution.py:18
  430.5 8.4 %collective-permute-start.17 = (f32[4,64,768]{2,1,0:T(8,128)S(1)}, f32[4,64,768]{2,1,0:T(8,128)S(1)}, u32[]{:S(2)}, u32[]{:S(2)}) collective-permute-start(f32[4,64,768]{2,1,0:T(8,128)S(1)} %add.248), channel_id=1, source_target_pairs={{0,8},{1,9},{2,10},{3,11},{4,12},{5,13},{6,14},{7,15},{8,16},{9,17... | collective-permute-start | bytes 2359304 | tf_op jit(solution)/shard_map/ppermute | solution.py:18
  438.9 12.9 %collective-permute-done.17 = f32[4,64,768]{2,1,0:T(8,128)S(1)} collective-permute-done((f32[4,64,768]{2,1,0:T(8,128)S(1)}, f32[4,64,768]{2,1,0:T(8,128)S(1)}, u32[]{:S(2)}, u32[]{:S(2)}) %collective-permute-start.17) | collective-permute-done | bytes 786464 | tf_op jit(solution)/shard_map/ppermute | solution.py:18
  452.0 13.2 %collective-permute-start.18 = (f32[4,64,768]{2,1,0:T(8,128)S(1)}, f32[4,64,768]{2,1,0:T(8,128)S(1)}, u32[]{:S(2)}, u32[]{:S(2)}) collective-permute-start(f32[4,64,768]{2,1,0:T(8,128)S(1)} %add.250), channel_id=1, source_target_pairs={{0,16},{1,17},{2,18},{3,19},{4,20},{5,21},{6,22},{7,23},{8,24},{9,... | collective-permute-start | bytes 2359304 | tf_op jit(solution)/shard_map/ppermute | solution.py:18
  465.2 15.2 %collective-permute-done.18 = f32[4,64,768]{2,1,0:T(8,128)S(1)} collective-permute-done((f32[4,64,768]{2,1,0:T(8,128)S(1)}, f32[4,64,768]{2,1,0:T(8,128)S(1)}, u32[]{:S(2)}, u32[]{:S(2)}) %collective-permute-start.18) | collective-permute-done | bytes 786464 | tf_op jit(solution)/shard_map/ppermute | solution.py:18
  488.2 13.9 %collective-permute-done.19 = f32[4,64,768]{2,1,0:T(8,128)S(1)} collective-permute-done((f32[4,64,768]{2,1,0:T(8,128)S(1)}, f32[4,64,768]{2,1,0:T(8,128)S(1)}, u32[]{:S(2)}, u32[]{:S(2)}) %collective-permute-start.19) | collective-permute-done | bytes 786464 | tf_op jit(solution)/shard_map/ppermute | solution.py:18
  508.1 12.8 %collective-permute-done.20 = f32[4,64,768]{2,1,0:T(8,128)S(1)} collective-permute-done((f32[4,64,768]{2,1,0:T(8,128)S(1)}, f32[4,64,768]{2,1,0:T(8,128)S(1)}, u32[]{:S(2)}, u32[]{:S(2)}) %collective-permute-start.20) | collective-permute-done | bytes 786464 | tf_op jit(solution)/shard_map/ppermute | solution.py:18
  521.3 27.8 %multiply_reduce_fusion = f32[4,64,768]{2,1,0:T(8,128)} fusion(f32[8]{0:T(128)S(1)} %copy-done.5, bf16[3072,768]{1,0:T(8,128)(2,1)} %param.8, f32[8,3072]{1,0:T(8,128)S(1)} %convert_element_type.32, f32[8,3072]{1,0:T(8,128)S(1)} %convert_add_fusion, bf16[768,3072]{1,0:T(8,128)(2,1)} %param.7, f32[8,4,64,768]{3,2,1,0:T(8,128)} %copy-done.1, ...), kind=kOutput, calls=%fused_computation.47 | convolution fusion | flops 19405799424 | bytes 23789600 | tf_op jit(solution)/shard_map/kbnd,dc->kbnc/dot_general | solution.py:31
  549.1 151.5 %all-reduce.2.cloned.1.call-done = f32[4,64,768]{2,1,0:T(8,128)} async-done(((f32[4,64,768]{2,1,0:T(8,128)}), f32[4,64,768]{2,1,0:T(8,128)}) %all-reduce.2.cloned.1.call-update) | async-done | bytes 786448 | tf_op jit(solution)/shard_map/psum | solution.py:37
  (65 shorter events, 86.0 us)
Async XLA Ops:
  6.5 694.1 %all-reduce.2.cloned.1.call-start = ((), (), s32[]{:S(2)}) async-start(), calls=%async_computation | async-start | bytes 1572864 | tf_op jit(solution)/shard_map/psum | solution.py:37
  6.5 6.0 slice-start
  8.6 4.0 slice-start.1
  12.6 29.8 %copy-start.5 = (f32[8]{0:T(128)S(1)}, f32[8]{0:T(128)}, u32[]{:S(2)}) copy-start(f32[8]{0:T(128)} %param.11) | copy-start | bytes 100
  42.4 2.6 copy-start.4
  45.1 81.7 %copy-start.2 = (f32[8,4,64,768]{3,2,1,0:T(8,128)}, f32[8,4,64,768]{3,2,1,0:T(8,128)S(1)}, u32[]{:S(2)}) copy-start(f32[8,4,64,768]{3,2,1,0:T(8,128)S(1)} %fusion.51) | copy-start | bytes 18874372
  45.1 13.4 %collective-permute-start = (f32[4,64,768]{2,1,0:T(8,128)S(1)}, f32[4,64,768]{2,1,0:T(8,128)S(1)}, u32[]{:S(2)}, u32[]{:S(2)}) collective-permute-start(f32[4,64,768]{2,1,0:T(8,128)S(1)} %slice_bitcast_fusion.2), channel_id=1, source_target_pairs={{0,1},{1,2},{2,3},{3,4},{4,5},{5,6},{6,7},{7,8},{8,9},{9,10},{10,1... | collective-permute-start | bytes 2359304 | tf_op jit(solution)/shard_map/ppermute | solution.py:18
  58.6 111.0 %copy-start = (f32[4,64,768]{2,1,0:T(8,128)S(1)}, f32[4,64,768]{2,1,0:T(8,128)}, u32[]{:S(2)}) copy-start(f32[4,64,768]{2,1,0:T(8,128)} %param.6) | copy-start | bytes 2359300
  58.6 18.7 %collective-permute-start.1 = (f32[4,64,768]{2,1,0:T(8,128)S(1)}, f32[4,64,768]{2,1,0:T(8,128)S(1)}, u32[]{:S(2)}, u32[]{:S(2)}) collective-permute-start(f32[4,64,768]{2,1,0:T(8,128)S(1)} %fusion.115), channel_id=1, source_target_pairs={{0,2},{1,3},{2,4},{3,5},{4,6},{5,7},{6,8},{7,9},{8,10},{9,11},{10,... | collective-permute-start | bytes 2359304 | tf_op jit(solution)/shard_map/ppermute | solution.py:18
  77.5 19.4 %collective-permute-start.2 = (f32[4,64,768]{2,1,0:T(8,128)S(1)}, f32[4,64,768]{2,1,0:T(8,128)S(1)}, u32[]{:S(2)}, u32[]{:S(2)}) collective-permute-start(f32[4,64,768]{2,1,0:T(8,128)S(1)} %add.210), channel_id=1, source_target_pairs={{0,4},{1,5},{2,6},{3,7},{4,8},{5,9},{6,10},{7,11},{8,12},{9,13},{1... | collective-permute-start | bytes 2359304 | tf_op jit(solution)/shard_map/ppermute | solution.py:18
  97.0 14.9 %collective-permute-start.3 = (f32[4,64,768]{2,1,0:T(8,128)S(1)}, f32[4,64,768]{2,1,0:T(8,128)S(1)}, u32[]{:S(2)}, u32[]{:S(2)}) collective-permute-start(f32[4,64,768]{2,1,0:T(8,128)S(1)} %add.212), channel_id=1, source_target_pairs={{0,8},{1,9},{2,10},{3,11},{4,12},{5,13},{6,14},{7,15},{8,16},{9,17... | collective-permute-start | bytes 2359304 | tf_op jit(solution)/shard_map/ppermute | solution.py:18
  112.0 14.7 %collective-permute-start.4 = (f32[4,64,768]{2,1,0:T(8,128)S(1)}, f32[4,64,768]{2,1,0:T(8,128)S(1)}, u32[]{:S(2)}, u32[]{:S(2)}) collective-permute-start(f32[4,64,768]{2,1,0:T(8,128)S(1)} %add.214), channel_id=1, source_target_pairs={{0,16},{1,17},{2,18},{3,19},{4,20},{5,21},{6,22},{7,23},{8,24},{9,... | collective-permute-start | bytes 2359304 | tf_op jit(solution)/shard_map/ppermute | solution.py:18
  126.8 23.5 %collective-permute-start.5 = (f32[4,64,768]{2,1,0:T(8,128)S(1)}, f32[4,64,768]{2,1,0:T(8,128)S(1)}, u32[]{:S(2)}, u32[]{:S(2)}) collective-permute-start(f32[4,64,768]{2,1,0:T(8,128)S(1)} %add.216), channel_id=1, source_target_pairs={{0,32},{1,33},{2,34},{3,35},{4,36},{5,37},{6,38},{7,39},{8,40},{9,... | collective-permute-start | bytes 2359304 | tf_op jit(solution)/shard_map/ppermute | solution.py:18
  150.4 19.2 %collective-permute-start.6 = (f32[4,64,768]{2,1,0:T(8,128)S(1)}, f32[4,64,768]{2,1,0:T(8,128)S(1)}, u32[]{:S(2)}, u32[]{:S(2)}) collective-permute-start(f32[4,64,768]{2,1,0:T(8,128)S(1)} %add.218), channel_id=1, source_target_pairs={{0,64},{1,65},{2,66},{3,67},{4,68},{5,69},{6,70},{7,71},{8,72},{9,... | collective-permute-start | bytes 2359304 | tf_op jit(solution)/shard_map/ppermute | solution.py:18
  202.1 98.9 %copy-start.3 = (f32[8,4,64,768]{3,2,1,0:T(8,128)}, f32[8,4,64,768]{3,2,1,0:T(8,128)S(1)}, u32[]{:S(2)}) copy-start(f32[8,4,64,768]{3,2,1,0:T(8,128)S(1)} %fusion.49) | copy-start | bytes 18874372
  202.2 23.4 %collective-permute-start.7 = (f32[4,64,768]{2,1,0:T(8,128)S(1)}, f32[4,64,768]{2,1,0:T(8,128)S(1)}, u32[]{:S(2)}, u32[]{:S(2)}) collective-permute-start(f32[4,64,768]{2,1,0:T(8,128)S(1)} %slice_bitcast_fusion.1), channel_id=1, source_target_pairs={{0,1},{1,2},{2,3},{3,4},{4,5},{5,6},{6,7},{7,8},{8,9},{9,10},{10,1... | collective-permute-start | bytes 2359304 | tf_op jit(solution)/shard_map/ppermute | solution.py:18
  225.7 15.7 %collective-permute-start.8 = (f32[4,64,768]{2,1,0:T(8,128)S(1)}, f32[4,64,768]{2,1,0:T(8,128)S(1)}, u32[]{:S(2)}, u32[]{:S(2)}) collective-permute-start(f32[4,64,768]{2,1,0:T(8,128)S(1)} %fusion.116), channel_id=1, source_target_pairs={{0,2},{1,3},{2,4},{3,5},{4,6},{5,7},{6,8},{7,9},{8,10},{9,11},{10,... | collective-permute-start | bytes 2359304 | tf_op jit(solution)/shard_map/ppermute | solution.py:18
  241.5 27.4 %collective-permute-start.9 = (f32[4,64,768]{2,1,0:T(8,128)S(1)}, f32[4,64,768]{2,1,0:T(8,128)S(1)}, u32[]{:S(2)}, u32[]{:S(2)}) collective-permute-start(f32[4,64,768]{2,1,0:T(8,128)S(1)} %add.228), channel_id=1, source_target_pairs={{0,4},{1,5},{2,6},{3,7},{4,8},{5,9},{6,10},{7,11},{8,12},{9,13},{1... | collective-permute-start | bytes 2359304 | tf_op jit(solution)/shard_map/ppermute | solution.py:18
  269.0 14.2 %collective-permute-start.10 = (f32[4,64,768]{2,1,0:T(8,128)S(1)}, f32[4,64,768]{2,1,0:T(8,128)S(1)}, u32[]{:S(2)}, u32[]{:S(2)}) collective-permute-start(f32[4,64,768]{2,1,0:T(8,128)S(1)} %add.230), channel_id=1, source_target_pairs={{0,8},{1,9},{2,10},{3,11},{4,12},{5,13},{6,14},{7,15},{8,16},{9,17... | collective-permute-start | bytes 2359304 | tf_op jit(solution)/shard_map/ppermute | solution.py:18
  283.3 17.7 %collective-permute-start.11 = (f32[4,64,768]{2,1,0:T(8,128)S(1)}, f32[4,64,768]{2,1,0:T(8,128)S(1)}, u32[]{:S(2)}, u32[]{:S(2)}) collective-permute-start(f32[4,64,768]{2,1,0:T(8,128)S(1)} %add.232), channel_id=1, source_target_pairs={{0,16},{1,17},{2,18},{3,19},{4,20},{5,21},{6,22},{7,23},{8,24},{9,... | collective-permute-start | bytes 2359304 | tf_op jit(solution)/shard_map/ppermute | solution.py:18
  301.1 18.8 %collective-permute-start.12 = (f32[4,64,768]{2,1,0:T(8,128)S(1)}, f32[4,64,768]{2,1,0:T(8,128)S(1)}, u32[]{:S(2)}, u32[]{:S(2)}) collective-permute-start(f32[4,64,768]{2,1,0:T(8,128)S(1)} %add.234), channel_id=1, source_target_pairs={{0,32},{1,33},{2,34},{3,35},{4,36},{5,37},{6,38},{7,39},{8,40},{9,... | collective-permute-start | bytes 2359304 | tf_op jit(solution)/shard_map/ppermute | solution.py:18
  320.0 18.5 %collective-permute-start.13 = (f32[4,64,768]{2,1,0:T(8,128)S(1)}, f32[4,64,768]{2,1,0:T(8,128)S(1)}, u32[]{:S(2)}, u32[]{:S(2)}) collective-permute-start(f32[4,64,768]{2,1,0:T(8,128)S(1)} %add.236), channel_id=1, source_target_pairs={{0,64},{1,65},{2,66},{3,67},{4,68},{5,69},{6,70},{7,71},{8,72},{9,... | collective-permute-start | bytes 2359304 | tf_op jit(solution)/shard_map/ppermute | solution.py:18
  370.9 109.6 %copy-start.1 = (f32[8,4,64,768]{3,2,1,0:T(8,128)}, f32[8,4,64,768]{3,2,1,0:T(8,128)S(1)}, u32[]{:S(2)}) copy-start(f32[8,4,64,768]{3,2,1,0:T(8,128)S(1)} %fusion.47) | copy-start | bytes 18874372
  371.0 28.2 %collective-permute-start.14 = (f32[4,64,768]{2,1,0:T(8,128)S(1)}, f32[4,64,768]{2,1,0:T(8,128)S(1)}, u32[]{:S(2)}, u32[]{:S(2)}) collective-permute-start(f32[4,64,768]{2,1,0:T(8,128)S(1)} %slice_bitcast_fusion), channel_id=1, source_target_pairs={{0,1},{1,2},{2,3},{3,4},{4,5},{5,6},{6,7},{7,8},{8,9},{9,10},{10,1... | collective-permute-start | bytes 2359304 | tf_op jit(solution)/shard_map/ppermute | solution.py:18
  399.2 14.9 %collective-permute-start.15 = (f32[4,64,768]{2,1,0:T(8,128)S(1)}, f32[4,64,768]{2,1,0:T(8,128)S(1)}, u32[]{:S(2)}, u32[]{:S(2)}) collective-permute-start(f32[4,64,768]{2,1,0:T(8,128)S(1)} %fusion.117), channel_id=1, source_target_pairs={{0,2},{1,3},{2,4},{3,5},{4,6},{5,7},{6,8},{7,9},{8,10},{9,11},{10,... | collective-permute-start | bytes 2359304 | tf_op jit(solution)/shard_map/ppermute | solution.py:18
  414.3 16.2 %collective-permute-start.16 = (f32[4,64,768]{2,1,0:T(8,128)S(1)}, f32[4,64,768]{2,1,0:T(8,128)S(1)}, u32[]{:S(2)}, u32[]{:S(2)}) collective-permute-start(f32[4,64,768]{2,1,0:T(8,128)S(1)} %add.246), channel_id=1, source_target_pairs={{0,4},{1,5},{2,6},{3,7},{4,8},{5,9},{6,10},{7,11},{8,12},{9,13},{1... | collective-permute-start | bytes 2359304 | tf_op jit(solution)/shard_map/ppermute | solution.py:18
  430.5 21.3 %collective-permute-start.17 = (f32[4,64,768]{2,1,0:T(8,128)S(1)}, f32[4,64,768]{2,1,0:T(8,128)S(1)}, u32[]{:S(2)}, u32[]{:S(2)}) collective-permute-start(f32[4,64,768]{2,1,0:T(8,128)S(1)} %add.248), channel_id=1, source_target_pairs={{0,8},{1,9},{2,10},{3,11},{4,12},{5,13},{6,14},{7,15},{8,16},{9,17... | collective-permute-start | bytes 2359304 | tf_op jit(solution)/shard_map/ppermute | solution.py:18
  452.0 28.4 %collective-permute-start.18 = (f32[4,64,768]{2,1,0:T(8,128)S(1)}, f32[4,64,768]{2,1,0:T(8,128)S(1)}, u32[]{:S(2)}, u32[]{:S(2)}) collective-permute-start(f32[4,64,768]{2,1,0:T(8,128)S(1)} %add.250), channel_id=1, source_target_pairs={{0,16},{1,17},{2,18},{3,19},{4,20},{5,21},{6,22},{7,23},{8,24},{9,... | collective-permute-start | bytes 2359304 | tf_op jit(solution)/shard_map/ppermute | solution.py:18
  480.5 21.5 %collective-permute-start.19 = (f32[4,64,768]{2,1,0:T(8,128)S(1)}, f32[4,64,768]{2,1,0:T(8,128)S(1)}, u32[]{:S(2)}, u32[]{:S(2)}) collective-permute-start(f32[4,64,768]{2,1,0:T(8,128)S(1)} %add.252), channel_id=1, source_target_pairs={{0,32},{1,33},{2,34},{3,35},{4,36},{5,37},{6,38},{7,39},{8,40},{9,... | collective-permute-start | bytes 2359304 | tf_op jit(solution)/shard_map/ppermute | solution.py:18
  502.2 18.7 %collective-permute-start.20 = (f32[4,64,768]{2,1,0:T(8,128)S(1)}, f32[4,64,768]{2,1,0:T(8,128)S(1)}, u32[]{:S(2)}, u32[]{:S(2)}) collective-permute-start(f32[4,64,768]{2,1,0:T(8,128)S(1)} %add.254), channel_id=1, source_target_pairs={{0,64},{1,65},{2,66},{3,67},{4,68},{5,69},{6,70},{7,71},{8,72},{9,... | collective-permute-start | bytes 2359304 | tf_op jit(solution)/shard_map/ppermute | solution.py:18
Sparse Core Ops, SparseCore 0:
  549.2 151.3 all-reduce.1
where the time goes:
time: 713 us; the launch traced here: 710 us
  waiting for transfers between devices  419 us (59%)
  starting transfers between devices  141 us (20%)
  matrix products  119 us (17%)
  other arithmetic  15.3 us (2%)
  between operations  14 us (2%)
    ppermute x21, waiting for transfers between devices, prefix_of(): received = lax.ppermute(inclusive, 'time', send_pairs)  268 us
    psum x1, waiting for transfers between devices, local_run(): result = x_init + lax.psum(jnp.sum(drifts, axis=0), 'time')  152 us
    ppermute x21, starting transfers between devices, prefix_of(): received = lax.ppermute(inclusive, 'time', send_pairs)  141 us
    dot_general x4, matrix products, local_run(): jnp.einsum('kbnd,dc->kbnc', hidden_act, w_out, preferred_element_type=jnp...  114 us
  transfers between devices with their start and end apart: 22, of which 22 were waited for; matrix products, arithmetic and copies ran while one was open for 0% of the time, Pallas kernels for 0%

commit v1 on v0

v1 whole, which is shorter than its diff:
```python
import math

import jax
import jax.numpy as jnp
from jax import lax
from jax.experimental import pallas as pl
from jax.experimental.pallas import tpu as pltpu
from jax.sharding import PartitionSpec as P

C = 768; D = 3072; T = 1024
K0 = math.sqrt(2.0 / math.pi)
K1 = 2.0 * K0
K3 = 8.0 * 0.044715 * K0
f32 = jnp.float32; bf16 = jnp.bfloat16

def gelu_half(w):
    u = w * (K1 + K3 * (w * w))
    return w * jnp.tanh(u) + w

def make(J=64, CH=1024, LAG=2):
    NB = T // J
    NCH = D // CH
    SUB = 256
    PC = C // NCH
    RING = 3 * LAG + 1
    M = 2 * J

    def kernel(x0_ref, win_ref, wout_ref, gam_ref, bet_ref, h_ref, y_ref,
               g_ring, b_ring, xs, fs, a0, rs, s_acc):
        rowid = lax.broadcasted_iota(jnp.int32, (8, PC), 0)
        xpad = jnp.concatenate([x0_ref[...], jnp.zeros((14, C), f32)], 0).astype(bf16)
        a0[...] = jnp.dot(xpad, win_ref[...], preferred_element_type=f32)[0:8]
        for s in range(3):
            for k in range(2):
                rs[s, k] = jnp.broadcast_to(x0_ref[k:k + 1, :], (8, C))
        s_acc[...] = jnp.zeros_like(s_acc)

        def body(t, n, act, pre):
            par = lax.rem(t, 2)
            off = n * CH
            if pre:
                pcol = pl.ds(pl.multiple_of(n * PC, PC), PC)
                for s in pre:
                    blk = t - 1 - LAG * s
                    for k in range(2):
                        carry = rs[s, k, :, pcol]
                        for p in range(J // 8):
                            r0 = k * J + p * 8
                            hv = h_ref[pl.ds(pl.multiple_of(blk * J, J) + p * 8, 8), :]
                            v = fs[1 - par, s, pl.ds(r0, 8), pcol] * jnp.concatenate([hv] * (PC // 128), 1)
                            c = v
                            for sh in (1, 2, 4):
                                c = c + jnp.where(rowid >= sh, pltpu.roll(c, sh, 0), 0.0)
                            fs[1 - par, s, pl.ds(r0, 8), pcol] = carry + (c - v)
                            carry = carry + jnp.broadcast_to(c[7:8, :], (8, PC))
                        rs[s, k, :, pcol] = carry
                        xs[1 - par, pl.ds((s * 2 + k) * J, J), pcol] = fs[1 - par, s, pl.ds(k * J, J), pcol].astype(bf16)
            mm = [s for s in act if s >= 1]
            outs = [s for s in act if s <= 2]
            slot = {s: lax.rem(t - LAG * s, RING) for s in act}
            gparts = []
            facc = None
            for i in range(CH // SUB):
                cols = pl.ds(pl.multiple_of(off + i * SUB, SUB), SUB)
                A = None
                if mm:
                    lo = (mm[0] - 1) * M; hi = mm[-1] * M
                    A = jnp.dot(xs[par, lo:hi, :], win_ref[:, cols], preferred_element_type=f32)
                gs = []
                for s in act:
                    if s == 0:
                        rows = pl.ds(pl.multiple_of(t * J, J), J)
                        g1 = gam_ref[rows, cols].astype(f32) * 0.5 + 0.5
                        b1 = bet_ref[rows, cols].astype(f32) * 0.5
                        g_ring[slot[0], :, cols] = g1
                        b_ring[slot[0], :, cols] = b1
                        for k in range(2):
                            ak = a0[k:k + 1, cols]
                            gs.append(gelu_half(ak * g1 + b1).astype(bf16))
                    else:
                        g1 = g_ring[slot[s], :, cols]
                        b1 = b_ring[slot[s], :, cols]
                        base = (s - mm[0]) * M
                        for k in range(2):
                            ak = A[base + k * J: base + (k + 1) * J]
                            gv = gelu_half(ak * g1 + b1).astype(bf16)
                            if s <= 2:
                                gs.append(gv)
                            else:
                                blk = t - LAG * 3
                                tot = s_acc[k, :, cols]
                                for p in range(J // 8):
                                    hv = h_ref[pl.ds(pl.multiple_of(blk * J, J) + p * 8, 8), :]
                                    tot = tot + gv[p * 8:(p + 1) * 8].astype(f32) * jnp.concatenate([hv] * (SUB // 128), 1)
                                s_acc[k, :, cols] = tot
                if outs:
                    G = jnp.concatenate(gs, 0) if len(gs) > 1 else gs[0]
                    gparts.append(G)
            if outs:
                G = jnp.concatenate(gparts, 1) if len(gparts) > 1 else gparts[0]
                d = jnp.dot(G, wout_ref[pl.ds(pl.multiple_of(off, CH), CH), :], preferred_element_type=f32)
                for q, s in enumerate(outs):
                    part = d[q * M:(q + 1) * M]

                    @pl.when(n == 0)
                    def _(): fs[par, s] = part

                    @pl.when(n != 0)
                    def _(): fs[par, s] += part

        nsteps = NB + 3 * LAG
        def sets(t):
            act = tuple(s for s in range(4) if 0 <= t - LAG * s < NB)
            pre = tuple(s for s in range(3) if 0 <= t - 1 - LAG * s < NB)
            return act, pre
        t = 0
        while t < nsteps:
            e = t
            while e < nsteps and sets(e) == sets(t):
                e += 1
            act, pre = sets(t)
            if e - t == 1:
                lax.fori_loop(0, NCH, lambda n, _, t=t, act=act, pre=pre: (body(jnp.int32(t), n, act, pre), 0)[1], 0)
            else:
                lax.fori_loop(0, NCH * (e - t), lambda i, _, t=t, act=act, pre=pre: (body(t + i // NCH, i % NCH, act, pre), 0)[1], 0)
            t = e

        st = jnp.concatenate([jnp.sum(s_acc[k], axis=0, keepdims=True) for k in range(2)], 0)
        h1 = st.astype(bf16); r1 = st - h1.astype(f32)
        h2 = r1.astype(bf16); r2 = r1 - h2.astype(f32)
        h3 = r2.astype(bf16)
        lhs = jnp.concatenate([h1.astype(f32), h2.astype(f32), h3.astype(f32), jnp.zeros((10, D), f32)], 0).astype(bf16)
        o = jnp.dot(lhs, wout_ref[...], preferred_element_type=f32)
        y_ref[...] = x0_ref[...] + (o[0:2] + (o[2:4] + o[4:6]))

    scratch = [
        pltpu.VMEM((RING, J, D), f32), pltpu.VMEM((RING, J, D), f32),
        pltpu.VMEM((2, 3 * M, C), bf16), pltpu.VMEM((2, 3, M, C), f32),
        pltpu.VMEM((8, D), f32), pltpu.VMEM((3, 2, 8, C), f32), pltpu.VMEM((2, 8, D), f32),
    ]
    return pl.pallas_call(kernel, out_shape=jax.ShapeDtypeStruct((2, C), f32),
        in_specs=[pl.BlockSpec(memory_space=pltpu.VMEM)] * 6,
        out_specs=pl.BlockSpec(memory_space=pltpu.VMEM),
        scratch_shapes=scratch,
        compiler_params=pltpu.CompilerParams(vmem_limit_bytes=62 * 2**20))


def solution(mesh):
    run = make()

    def local_run(x_init, w_in, w_out, mod_gamma, mod_beta, step_size):
        me = lax.axis_index("time")
        x2 = lax.dynamic_slice(x_init.reshape(256, C), (2 * me, 0), (2, C))
        gam = lax.all_gather(mod_gamma, "time", axis=0, tiled=True)
        bet = lax.all_gather(mod_beta, "time", axis=0, tiled=True)
        h = lax.all_gather(step_size, "time", axis=0, tiled=True)
        hb = jnp.broadcast_to(h[:, None], (T, 128))
        y2 = run(x2, w_in, w_out, gam, bet, hb)
        y = lax.all_gather(y2, "time", axis=0, tiled=True)
        return y.reshape(x_init.shape)

    return jax.shard_map(local_run, mesh=mesh, in_specs=(P("data", None, None), P(None, None), P(None, None), P("time", None), P("time", None), P("time")), out_specs=P("data", None, None), check_vma=False)
```

time: 713 us -> 312 us (0.44)
  waiting for transfers between devices: 419 us -> 74.2 us
  starting transfers between devices: 141 us -> 0.04 us
  matrix products: 119 us -> 0 us
  Pallas kernels: 0 us -> 117 us
  blocking collectives: 0 us -> 103 us
  other arithmetic: 15.3 us -> 0 us
    ppermute x21 -> x0, waiting for transfers between devices: 268 us -> none  [prefix_of(): received = lax.ppermute(inclusive, 'time', send_pairs)]
    psum x1 -> x0, waiting for transfers between devices: 152 us -> none  [local_run(): result = x_init + lax.psum(jnp.sum(drifts, axis=0), 'time')]
    ppermute x21 -> x0, starting transfers between devices: 141 us -> none  [prefix_of(): received = lax.ppermute(inclusive, 'time', send_pairs)]
    dot_general x5 -> x0, matrix products: 119 us -> none  [the longest x4 114 us: local_run(): jnp.einsum('kbnd,dc->kbnc', hidden_act, w_out, preferred_element_type=jnp...]
    pallas_call x0 -> x1, Pallas kernels: none -> 117 us  [local_run(): y2 = run(x2, w_in, w_out, gam, bet, hb)]
    all_gather x0 -> x2, waiting for transfers between devices: none -> 72.8 us  [the longest x1 68.7 us: local_run(): bet = lax.all_gather(mod_beta, 'time', axis=0, tiled=True)]
    unnamed x0 -> x1, blocking collectives: none -> 69.2 us
    all_gather x0 -> x1, blocking collectives: none -> 34 us  [local_run(): y = lax.all_gather(y2, 'time', axis=0, tiled=True)]
  transfers between devices with their start and end apart: 22 -> 2, of which waited for: 22 -> 2; matrix products, arithmetic and copies ran while one was open for 0% -> 0% of each run, Pallas kernels for 0% -> 0%
where the time goes in v1:
time: 312 us; the launch traced here: 311 us
  Pallas kernels  117 us (38%)
  blocking collectives  103 us (33%)
  waiting for transfers between devices  74.2 us (24%)
  between operations  13.4 us (4%)
  local copies, waits for them, and re-layouts  3.88 us (1%)
    pallas_call x1, Pallas kernels, local_run(): y2 = run(x2, w_in, w_out, gam, bet, hb)  117 us
    unnamed x1, blocking collectives  69.2 us
    all_gather x1, waiting for transfers between devices, local_run(): bet = lax.all_gather(mod_beta, 'time', axis=0, tiled=True)  68.7 us
    all_gather x1, blocking collectives, local_run(): y = lax.all_gather(y2, 'time', axis=0, tiled=True)  34 us
  transfers between devices with their start and end apart: 2, of which 2 were waited for; matrix products, arithmetic and copies ran while one was open for 0% of the time, Pallas kernels for 0%

profile of v1, /device:TPU:1, one launch (start us, length us, event | category | flops | bytes accessed | tf_op | source)
XLA Modules:
  0.0 311.3 jit_solution(17110905042241268507)
XLA Ops:
  6.5 0.0 copy-start
  6.5 0.0 all-gather.4.cloned.1.call-start
  6.5 0.7 all-gather.4.cloned.1.call-update
  7.3 0.0 all-gather.6.cloned.1.call-start
  7.3 0.7 all-gather.6.cloned.1.call-update
  8.0 0.9 dynamic-update-slice
  8.9 69.2 %all-reduce = f32[1024]{0:T(1024)S(1)} all-reduce(f32[1024]{0:T(1024)S(1)} %dynamic-update-slice), channel_id=1, replica_groups=mesh['data'=1,'time'=128] {'time'}, use_global_device_ids=true, to_apply=%add | all-reduce | flops 1024 | bytes 8192
  78.1 0.0 copy-done
  78.1 0.6 constant_dynamic-slice_fusion.x0_ref
  78.7 4.1 %all-gather.4.cloned.1.call-done.gam_ref = bf16[1024,3072]{1,0:T(8,128)(2,1)} async-done(((bf16[8,3072]{1,0:T(8,128)(2,1)}), bf16[1024,3072]{1,0:T(8,128)(2,1)}) %all-gather.4.cloned.1.call-update) | async-done | bytes 6291472 | tf_op jit(solution)/shard_map/all_gather | solution.py:154
  82.8 68.7 %all-gather.6.cloned.1.call-done.bet_ref = bf16[1024,3072]{1,0:T(8,128)(2,1)} async-done(((bf16[8,3072]{1,0:T(8,128)(2,1)}), bf16[1024,3072]{1,0:T(8,128)(2,1)}) %all-gather.6.cloned.1.call-update) | async-done | bytes 6291472 | tf_op jit(solution)/shard_map/all_gather | solution.py:155
  151.5 1.0 broadcast_in_dim.2.h_ref
  152.5 116.6 %shard_map.64 = f32[2,768]{1,0:T(2,128)} custom-call(f32[2,768]{1,0:T(2,128)} %constant_dynamic-slice_fusion.x0_ref, bf16[768,3072]{1,0:T(8,128)(2,1)} %win_ref.1, bf16[3072,768]{1,0:T(8,128)(2,1)} %wout_ref.1, bf16[1024,3072]{1,0:T(8,128)(2,1)} %all-gather.4.cloned.1.call-done.gam_ref, bf16[1024,3072]{1,0:T(8,128)(2,1)} %all-gather.6.cloned.1.call-done.bet_ref, ...), custom_call_target="tpu_custom_call" | custom-call | tf_op jit(solution)/shard_map/pallas_call | solution.py:158
  269.1 34.0 %all-gather = f32[128,2,768]{2,1,0:T(2,128)S(1)} all-gather(f32[1,2,768]{2,1,0:T(2,128)} %bitcast.3), channel_id=1, replica_groups=mesh['data'=1,'time'=128] {'time'}, dimensions={0}, use_global_device_ids=true | all-gather | bytes 792576 | tf_op jit(solution)/shard_map/all_gather | solution.py:159
  303.0 1.4 reshape.8
  (1 shorter events, 0.0 us)
Async XLA Ops:
  6.5 71.5 %copy-start = (f32[4,64,768]{2,1,0:T(8,128)S(1)}, f32[4,64,768]{2,1,0:T(8,128)}, u32[]{:S(2)}) copy-start(f32[4,64,768]{2,1,0:T(8,128)} %param.6) | copy-start | bytes 2359300
  6.5 76.3 %all-gather.4.cloned.1.call-start = ((), (), s32[]{:S(2)}) async-start(), calls=%async_computation | async-start | bytes 6340608 | tf_op jit(solution)/shard_map/all_gather | solution.py:154
  7.3 144.2 %all-gather.6.cloned.1.call-start = ((), (), s32[]{:S(2)}) async-start(), calls=%async_computation.1 | async-start | bytes 6340608 | tf_op jit(solution)/shard_map/all_gather | solution.py:155
Sparse Core Ops, SparseCore 0:
  10.4 72.3 all-gather.3
  85.9 65.5 all-gather.5

commit v2 on v0

v2 whole, which is shorter than its diff:
```python
import math

import jax
import jax.numpy as jnp
from jax import lax
from jax.experimental import pallas as pl
from jax.experimental.pallas import tpu as pltpu
from jax.sharding import PartitionSpec as P

C = 768
D = 3072
T = 1024
J = 64
CH = 1024
LAG = 2
D2LAG = 2
SUB = 256
NB = T // J
NCH = D // CH
NS = CH // SUB
PC = C // NCH
RING = 3 * LAG + 1
M = 2 * J
K0 = math.sqrt(2.0 / math.pi)
K1 = 2.0 * K0
K3 = 8.0 * 0.044715 * K0
f32 = jnp.float32
bf16 = jnp.bfloat16


def gelu_half(w):
    return w * jnp.tanh(w * (K1 + K3 * (w * w))) + w


def kernel(x_hbm, win_hbm, wout_hbm, gam_hbm, bet_hbm, h_hbm, y_ref,
           gb, hb, win_ref, wout_ref, x8, g_ring, b_ring, xs0, xs1, fs0, fs1, a0, rs, s_acc, yall,
           local_sem, send_sem, sendh_sem, in_sem, inh_sem, x_sem, xh_sem, d_sem, dh_sem, ysend_sem, y_sem):
    me = lax.axis_index("time")
    c = lax.rem(me, 2)
    x = lax.rem(me // 2, 4)
    y = lax.rem(me // 8, 4)
    z = me // 32

    def peer(zz, yy, xx, cc):
        return {"time": ((zz * 4 + yy) * 4 + xx) * 2 + cc}

    def chip(zz, yy, xx):
        return (zz * 4 + yy) * 4 + xx

    mychip = chip(z, y, x)
    zpeers = [peer(lax.rem(z + d, 4), y, x, c) for d in (1, 3, 2)]
    ypeers = [peer(z, lax.rem(y + d, 4), x, c) for d in (1, 3, 2)]
    xpeers = [peer(z, y, lax.rem(x + d, 4), c) for d in (1, 3, 2)]
    partner = peer(z, y, x, 1 - c)

    own = [pltpu.make_async_copy(gam_hbm, gb.at[mychip, c, 0], local_sem.at[0]),
           pltpu.make_async_copy(bet_hbm, gb.at[mychip, c, 1], local_sem.at[1]),
           pltpu.make_async_copy(h_hbm, hb.at[mychip, c], local_sem.at[2])]
    weights = [pltpu.make_async_copy(x_hbm.at[pl.ds(pl.multiple_of((me // 4) * 8, 8), 8)], x8, local_sem.at[3]),
               pltpu.make_async_copy(win_hbm, win_ref, local_sem.at[4]),
               pltpu.make_async_copy(wout_hbm, wout_ref, local_sem.at[5])]
    for cp in own + weights:
        cp.start()

    barrier = pltpu.get_barrier_semaphore()
    for p in zpeers + ypeers + xpeers + [partner]:
        pl.semaphore_signal(barrier, inc=1, device_id=p, device_id_type=pl.DeviceIdType.MESH)
    pl.semaphore_wait(barrier, 10)
    for cp in own:
        cp.wait()

    def send(src, dst, ssem, rsem, dev):
        pltpu.make_async_remote_copy(src_ref=src, dst_ref=dst, send_sem=ssem, recv_sem=rsem,
                                     device_id=dev, device_id_type=pl.DeviceIdType.MESH).start()

    def send_chunk(q, cc, peers, gsem, hsem):
        for p in peers:
            send(gb.at[q, cc], gb.at[q, cc], send_sem, gsem, p)
            send(hb.at[q, cc], hb.at[q, cc], sendh_sem, hsem, p)

    def wait_chunks(n, gsem, hsem):
        g = gb.at[pl.ds(0, n), 0]
        h = hb.at[pl.ds(0, n), 0]
        pltpu.make_async_copy(g, g, gsem).wait()
        pltpu.make_async_copy(h, h, hsem).wait()

    def stage_z():
        b = z * 4 + y
        send_chunk(mychip, c, zpeers, in_sem.at[b], inh_sem.at[b])

    def stage_y(z0):
        b = z0 * 4 + y

        @pl.when(z != z0)
        def _():
            wait_chunks(1, in_sem.at[b], inh_sem.at[b])
        send_chunk(chip(z0, y, x), c, ypeers, in_sem.at[b], inh_sem.at[b])

    def stage_x(b):
        y0 = lax.rem(b, 4)

        @pl.when(y != y0)
        def _():
            wait_chunks(1, in_sem.at[b], inh_sem.at[b])
        send_chunk(b * 4 + x, c, xpeers, x_sem.at[b], xh_sem.at[b])

    def stage_d(b):
        wait_chunks(3, x_sem.at[b], xh_sem.at[b])
        g = gb.at[pl.ds(b * 4, 4), c]
        h = hb.at[pl.ds(b * 4, 4), c]
        send(g, g, send_sem, d_sem.at[b], partner)
        send(h, h, sendh_sem, dh_sem.at[b], partner)

    def arrive(b):
        wait_chunks(4, d_sem.at[b], dh_sem.at[b])

    stage_z()
    for cp in weights:
        cp.wait()
    x2 = x8[0:2, :]
    for i in range(1, 4):
        x2 = jnp.where(lax.rem(me, 4) == i, x8[2 * i:2 * i + 2, :], x2)
    rowid = lax.broadcasted_iota(jnp.int32, (8, PC), 0)
    xpad = jnp.concatenate([x2, jnp.zeros((14, C), f32)], 0).astype(bf16)
    a0[...] = jnp.dot(xpad, win_ref[...], preferred_element_type=f32)[0:8]
    for s in range(3):
        for k in range(2):
            rs[s, k] = jnp.broadcast_to(x2[k:k + 1, :], (8, C))
    s_acc[...] = jnp.zeros_like(s_acc)
    fs0[...] = jnp.zeros_like(fs0)
    fs1[...] = jnp.zeros_like(fs1)
    XS = (xs0, xs1)
    FS = (fs0, fs1)
    zero = jnp.zeros((8, PC), f32)

    def hrows(blk, p):
        return hb[blk * 4 + p // 2, p % 2]

    def body(t, par, n, act, pre):
        off = n * CH
        fcur, fprev, xcur, xnext = FS[par], FS[1 - par], XS[par], XS[1 - par]
        pcol = pl.ds(pl.multiple_of(n * PC, PC), PC)

        def prefix(s, k):
            blk = t - 1 - LAG * s
            carry = rs[s, k, :, pcol]
            for p2 in range(J // 16):
                xr = []
                for p in (2 * p2, 2 * p2 + 1):
                    r0 = k * J + p * 8
                    v = fprev[s, pl.ds(r0, 8), pcol] * jnp.concatenate([hrows(blk, p)] * (PC // 128), 1)
                    fprev[s, pl.ds(r0, 8), pcol] = zero
                    cum = v
                    for sh in (1, 2, 4):
                        cum = cum + jnp.where(rowid >= sh, pltpu.roll(cum, sh, 0), 0.0)
                    xr.append(carry + (cum - v))
                    carry = carry + jnp.broadcast_to(cum[7:8, :], (8, PC))
                xnext[pl.ds((s * 2 + k) * J + p2 * 16, 16), pcol] = jnp.concatenate(xr, 0).astype(bf16)
            rs[s, k, :, pcol] = carry

        pieces = [(s, k) for s in pre for k in range(2)]
        mm = [s for s in act if s >= 1]
        outs = [s for s in act if s <= 2]
        slot = {s: lax.rem(t - LAG * s, RING) for s in act}
        G = [None] * NS
        acc = None

        def columns(i):
            return pl.ds(pl.multiple_of(off + i * SUB, SUB), SUB)

        def d1(i):
            lo, hi = (mm[0] - 1) * M, mm[-1] * M
            return jnp.dot(xcur[lo:hi, :], win_ref[:, columns(i)], preferred_element_type=f32)

        def gelus(i, A):
            cols = columns(i)
            gs = []
            for s in act:
                if s == 0:
                    chips = pl.ds(t * 4, 4)
                    g1 = gb[chips, :, 0, :, cols].astype(f32).reshape(J, SUB) * 0.5 + 0.5
                    b1 = gb[chips, :, 1, :, cols].astype(f32).reshape(J, SUB) * 0.5
                    g_ring[slot[0], :, cols] = g1
                    b_ring[slot[0], :, cols] = b1
                    for k in range(2):
                        gs.append(gelu_half(a0[k:k + 1, cols] * g1 + b1).astype(bf16))
                else:
                    g1 = g_ring[slot[s], :, cols]
                    b1 = b_ring[slot[s], :, cols]
                    base = (s - mm[0]) * M
                    for k in range(2):
                        ak = A[base + k * J: base + (k + 1) * J]
                        gv = gelu_half(ak * g1 + b1).astype(bf16)
                        if s <= 2:
                            gs.append(gv)
                        else:
                            blk = t - LAG * 3
                            tot = s_acc[k, :, cols]
                            for p in range(J // 8):
                                tot = tot + gv[p * 8:(p + 1) * 8].astype(f32) * jnp.concatenate([hrows(blk, p)] * (SUB // 128), 1)
                            s_acc[k, :, cols] = tot
            if outs:
                return jnp.concatenate(gs, 0) if len(gs) > 1 else gs[0]

        def d2(i):
            return jnp.dot(G[i], wout_ref[columns(i), :], preferred_element_type=f32)

        np_ = len(pieces)
        for i in range(NS):
            A = d1(i) if mm else None
            G[i] = gelus(i, A)
            if outs and i >= D2LAG:
                r = d2(i - D2LAG)
                acc = r if acc is None else acc + r
            for (s, k) in pieces[np_ * i // NS: np_ * (i + 1) // NS]:
                prefix(s, k)
        if outs:
            for i in range(NS - D2LAG, NS):
                r = d2(i)
                acc = r if acc is None else acc + r
            for q, s in enumerate(outs):
                fcur[s] += acc[q * M:(q + 1) * M]

    def sets(t):
        act = tuple(s for s in range(4) if 0 <= t - LAG * s < NB)
        pre = tuple(s for s in range(3) if 0 <= t - 1 - LAG * s < NB)
        return act, pre

    def when(cond, fn, arg):
        if isinstance(cond, bool):
            if cond:
                fn(arg)
        else:
            pl.when(cond)(lambda: fn(arg))

    def step(t, par, act, pre):
        when(t + 2 < NB, stage_x, t + 2)
        when(t + 1 < NB, stage_d, t + 1)
        when(t < NB, arrive, t)
        lax.fori_loop(0, NCH, lambda n, _: (body(t, par, n, act, pre), 0)[1], 0)

    stage_y(0)
    stage_x(0)
    stage_y(1)
    stage_x(1)
    stage_d(0)
    nsteps = NB + 3 * LAG
    t = 0
    while t < nsteps:
        e = t
        while e < nsteps and sets(e) == sets(t):
            e += 1
        act, pre = sets(t)
        if e - t >= 4:
            def pair(u, _, t=t, act=act, pre=pre):
                for q in range(2):
                    step(t + 2 * u + q, (t + q) % 2, act, pre)
                return 0
            lax.fori_loop(0, (e - t) // 2, pair, 0)
        else:
            for tt in range(t, e):
                if tt in (1, 3):
                    stage_y(2 + tt // 2)
                step(tt, tt % 2, act, pre)
        t = e

    st = jnp.concatenate([jnp.sum(s_acc[k], axis=0, keepdims=True) for k in range(2)], 0)
    h1 = st.astype(bf16).astype(f32)
    h2 = (st - h1).astype(bf16).astype(f32)
    h3 = st - h1 - h2
    lhs = jnp.concatenate([h1, h2, h3, jnp.zeros((10, D), f32)], 0).astype(bf16)
    o = jnp.dot(lhs, wout_ref[...], preferred_element_type=f32)
    yall[z, y, x, c] = x2 + (o[0:2] + (o[2:4] + o[4:6]))

    def ysend(ref, i, peers):
        for p in peers:
            send(ref, ref, ysend_sem, y_sem.at[i], p)

    def ywait(i, shape_ref):
        pltpu.make_async_copy(shape_ref, shape_ref, y_sem.at[i]).wait()

    ysend(yall.at[z, y, x, c], 0, xpeers)
    ywait(0, yall.at[0, 0, pl.ds(0, 3), 0])
    ysend(yall.at[z, y, :, c], 1, ypeers)
    ywait(1, yall.at[0, pl.ds(0, 3), :, 0])
    ysend(yall.at[z, :, :, c], 2, zpeers)
    ywait(2, yall.at[pl.ds(0, 3), :, :, 0])
    ysend(yall.at[:, :, :, c], 3, [partner])
    ywait(3, yall.at[:, :, :, 0])
    for zz in range(4):
        for yy in range(4):
            for x2_ in range(2):
                rows = [yall[zz, yy, x2_ * 2 + i // 2, i % 2] for i in range(4)]
                y_ref[pl.ds((zz * 4 + yy) * 16 + x2_ * 8, 8), :] = jnp.concatenate(rows, 0)

    def drain(ref, sem):
        for view in (ref.at[pl.ds(0, 63), 0], ref.at[:, 0]):
            pltpu.make_async_copy(view, view, sem).wait()
    drain(gb, send_sem)
    drain(hb, sendh_sem)
    for view in (yall.at[pl.ds(0, 3), :, :, 0], yall.at[0, pl.ds(0, 3), :, 0], yall.at[0, 0, pl.ds(0, 3), 0], yall.at[:, :, :, 0]):
        pltpu.make_async_copy(view, view, ysend_sem).wait()


def solution(mesh):
    V = pltpu.VMEM
    dma = pltpu.SemaphoreType.DMA
    run = pl.pallas_call(
        kernel,
        out_shape=jax.ShapeDtypeStruct((256, C), f32),
        in_specs=[pl.BlockSpec(memory_space=pl.ANY)] * 6,
        out_specs=pl.BlockSpec(memory_space=pltpu.VMEM),
        scratch_shapes=[
            V((64, 2, 2, 8, D), bf16), V((64, 2, 8, 128), f32), V((C, D), bf16), V((D, C), bf16), V((8, C), f32),
            V((RING, J, D), f32), V((RING, J, D), f32),
            V((3 * M, C), bf16), V((3 * M, C), bf16), V((3, M, C), f32), V((3, M, C), f32),
            V((8, D), f32), V((3, 2, 8, C), f32), V((2, 8, D), f32), V((4, 4, 4, 2, 2, C), f32),
            dma((6,)), dma, dma, dma((NB,)), dma((NB,)), dma((NB,)), dma((NB,)), dma((NB,)), dma((NB,)), dma, dma((4,)),
        ],
        compiler_params=pltpu.CompilerParams(vmem_limit_bytes=60 * 2**20, collective_id=0, has_side_effects=True),
    )

    def local_run(x_init, w_in, w_out, mod_gamma, mod_beta, step_size):
        hb = jnp.broadcast_to(step_size[:, None], (8, 128))
        y = run(x_init.reshape(256, C), w_in, w_out, mod_gamma, mod_beta, hb)
        return y.reshape(x_init.shape)

    return jax.shard_map(local_run, mesh=mesh, in_specs=(P("data", None, None), P(None, None), P(None, None), P("time", None), P("time", None), P("time")), out_specs=P("data", None, None), check_vma=False)
```

time: 713 us -> 160 us (0.22)
  waiting for transfers between devices: 419 us -> 0 us
  Pallas kernels: 0 us -> 157 us
  starting transfers between devices: 141 us -> 0 us
  matrix products: 119 us -> 0 us
  other arithmetic: 15.3 us -> 0 us
  between operations: 14 us -> 0.01 us
    ppermute x21 -> x0, waiting for transfers between devices: 268 us -> none  [prefix_of(): received = lax.ppermute(inclusive, 'time', send_pairs)]
    pallas_call x0 -> x1, Pallas kernels: none -> 157 us  [local_run(): y = run(x_init.reshape(256, C), w_in, w_out, mod_gamma, mod_beta, hb)]
    psum x1 -> x0, waiting for transfers between devices: 152 us -> none  [local_run(): result = x_init + lax.psum(jnp.sum(drifts, axis=0), 'time')]
    ppermute x21 -> x0, starting transfers between devices: 141 us -> none  [prefix_of(): received = lax.ppermute(inclusive, 'time', send_pairs)]
    dot_general x5 -> x0, matrix products: 119 us -> none  [the longest x4 114 us: local_run(): jnp.einsum('kbnd,dc->kbnc', hidden_act, w_out, preferred_element_type=jnp...]
    another operation x3 -> x0, other arithmetic: 8.14 us -> none  [local_run(): running = jnp.cumsum(drifts, axis=0)]
  transfers between devices with their start and end apart: 22 -> 0, of which waited for: 22 -> 0; matrix products, arithmetic and copies ran while one was open for 0% -> 0% of each run, Pallas kernels for 0% -> 0%
where the time goes in v2:
time: 160 us
  Pallas kernels  157 us (98%)
  local copies, waits for them, and re-layouts  3.4 us (2%)
    pallas_call x1, Pallas kernels, local_run(): y = run(x_init.reshape(256, C), w_in, w_out, mod_gamma, mod_beta, hb)  157 us

profile of v2, /device:TPU:1, one launch (start us, length us, event | category | flops | bytes accessed | tf_op | source)
XLA Modules:
  0.0 160.3 jit_solution(17540759558168194662)
XLA Ops:
  0.0 1.3 broadcast_in_dim.2.h_hbm
  1.3 156.9 %shard_map.64 = f32[256,768]{1,0:T(8,128)} custom-call(f32[256,768]{1,0:T(8,128)} %bitcast.3, bf16[768,3072]{1,0:T(8,128)(2,1)} %win_hbm.1, bf16[3072,768]{1,0:T(8,128)(2,1)} %wout_hbm.1, bf16[8,3072]{1,0:T(8,128)(2,1)} %gam_hbm.1, bf16[8,3072]{1,0:T(8,128)(2,1)} %bet_hbm.1, f32[8,128]{1,0:T(8,128)} %broadcast_in_dim.2.h_hbm), custom_call_target="tpu_custom_call" | custom-call | tf_op jit(solution)/shard_map/pallas_call | solution.py:325
  158.2 2.1 %copy.8 = f32[4,64,768]{2,1,0:T(8,128)} copy(f32[4,64,768]{2,1,0:T(8,128)} %bitcast.2) | data formatting | bytes 1572864

commit v3 on v2

--- a/solution.py
+++ b/solution.py
@@ -32,7 +32,7 @@
     return w * jnp.tanh(w * (K1 + K3 * (w * w))) + w
 
 
-def kernel(x_hbm, win_hbm, wout_hbm, gam_hbm, bet_hbm, h_hbm, y_ref,
+def kernel(x_hbm, win_hbm, wout_hbm, gam_hbm, bet_hbm, h_smem, y_ref,
            gb, hb, win_ref, wout_ref, x8, g_ring, b_ring, xs0, xs1, fs0, fs1, a0, rs, s_acc, yall,
            local_sem, send_sem, sendh_sem, in_sem, inh_sem, x_sem, xh_sem, d_sem, dh_sem, ysend_sem, y_sem):
     me = lax.axis_index("time")
@@ -53,9 +53,11 @@
     xpeers = [peer(z, y, lax.rem(x + d, 4), c) for d in (1, 3, 2)]
     partner = peer(z, y, x, 1 - c)
 
+    for j in range(8):
+        hb[mychip, c, j:j + 1, :] = jnp.full((1, 128), h_smem[j], f32)
     own = [pltpu.make_async_copy(gam_hbm, gb.at[mychip, c, 0], local_sem.at[0]),
            pltpu.make_async_copy(bet_hbm, gb.at[mychip, c, 1], local_sem.at[1]),
-           pltpu.make_async_copy(h_hbm, hb.at[mychip, c], local_sem.at[2])]
+           ]
     weights = [pltpu.make_async_copy(x_hbm.at[pl.ds(pl.multiple_of((me // 4) * 8, 8), 8)], x8, local_sem.at[3]),
                pltpu.make_async_copy(win_hbm, win_ref, local_sem.at[4]),
                pltpu.make_async_copy(wout_hbm, wout_ref, local_sem.at[5])]
@@ -120,7 +122,7 @@
     x2 = x8[0:2, :]
     for i in range(1, 4):
         x2 = jnp.where(lax.rem(me, 4) == i, x8[2 * i:2 * i + 2, :], x2)
-    rowid = lax.broadcasted_iota(jnp.int32, (8, PC), 0)
+    rowid = lax.broadcasted_iota(jnp.int32, (8, 128), 0)
     xpad = jnp.concatenate([x2, jnp.zeros((14, C), f32)], 0).astype(bf16)
     a0[...] = jnp.dot(xpad, win_ref[...], preferred_element_type=f32)[0:8]
     for s in range(3):
@@ -131,10 +133,14 @@
     fs1[...] = jnp.zeros_like(fs1)
     XS = (xs0, xs1)
     FS = (fs0, fs1)
-    zero = jnp.zeros((8, PC), f32)
+
+    hflat = hb.reshape(T, 128)
 
     def hrows(blk, p):
         return hb[blk * 4 + p // 2, p % 2]
+
+    def hstrided(blk, p):
+        return hflat[pl.ds(pl.multiple_of(blk * J, J) + p, 8, stride=8), :]
 
     def body(t, par, n, act, pre):
         off = n * CH
@@ -143,20 +149,25 @@
 
         def prefix(s, k):
             blk = t - 1 - LAG * s
-            carry = rs[s, k, :, pcol]
-            for p2 in range(J // 16):
-                xr = []
-                for p in (2 * p2, 2 * p2 + 1):
-                    r0 = k * J + p * 8
-                    v = fprev[s, pl.ds(r0, 8), pcol] * jnp.concatenate([hrows(blk, p)] * (PC // 128), 1)
-                    fprev[s, pl.ds(r0, 8), pcol] = zero
-                    cum = v
-                    for sh in (1, 2, 4):
-                        cum = cum + jnp.where(rowid >= sh, pltpu.roll(cum, sh, 0), 0.0)
-                    xr.append(carry + (cum - v))
-                    carry = carry + jnp.broadcast_to(cum[7:8, :], (8, PC))
-                xnext[pl.ds((s * 2 + k) * J + p2 * 16, 16), pcol] = jnp.concatenate(xr, 0).astype(bf16)
-            rs[s, k, :, pcol] = carry
+            for cc in range(PC // 128):
+                lt = n * (PC // 128) + cc
+                lane = pl.ds(pl.multiple_of(n * PC, PC) + cc * 128, 128)
+                run = None
+                before = []
+                for p in range(8):
+                    v = fprev[s, lt, pl.ds(k * J + p, 8, stride=8), :] * hstrided(blk, p)
+                    before.append(run)
+                    run = v if run is None else run + v
+                cum = run
+                for sh in (1, 2, 4):
+                    cum = cum + jnp.where(rowid >= sh, pltpu.roll(cum, sh, 0), 0.0)
+                carry = rs[s, k, :, lane]
+                base = carry + (cum - run)
+                rs[s, k, :, lane] = carry + jnp.broadcast_to(cum[7:8, :], (8, 128))
+                for p in range(8):
+                    fprev[s, lt, pl.ds(k * J + p, 8, stride=8), :] = base if p == 0 else base + before[p]
+                xnext[pl.ds((s * 2 + k) * J, J), lane] = fprev[s, lt, pl.ds(k * J, J), :].astype(bf16)
+                fprev[s, lt, pl.ds(k * J, J), :] = jnp.zeros((J, 128), f32)
 
         pieces = [(s, k) for s in pre for k in range(2)]
         mm = [s for s in act if s >= 1]
@@ -219,7 +230,8 @@
                 r = d2(i)
                 acc = r if acc is None else acc + r
             for q, s in enumerate(outs):
-                fcur[s] += acc[q * M:(q + 1) * M]
+                for ct in range(C // 128):
+                    fcur[s, ct] += acc[q * M:(q + 1) * M, ct * 128:(ct + 1) * 128]
 
     def sets(t):
         act = tuple(s for s in range(4) if 0 <= t - LAG * s < NB)
@@ -234,15 +246,21 @@
             pl.when(cond)(lambda: fn(arg))
 
     def step(t, par, act, pre):
-        when(t + 2 < NB, stage_x, t + 2)
-        when(t + 1 < NB, stage_d, t + 1)
         when(t < NB, arrive, t)
-        lax.fori_loop(0, NCH, lambda n, _: (body(t, par, n, act, pre), 0)[1], 0)
+        when(t + 4 < NB, stage_x, t + 4)
+
+        def piece(n, _):
+            def mid(arg):
+                pl.when(n == 1)(lambda: stage_d(arg))
+            when(t + 1 < NB, mid, t + 1)
+            body(t, par, n, act, pre)
+            return 0
+        lax.fori_loop(0, NCH, piece, 0)
 
     stage_y(0)
-    stage_x(0)
+    for b in range(4):
+        stage_x(b)
     stage_y(1)
-    stage_x(1)
     stage_d(0)
     nsteps = NB + 3 * LAG
     t = 0
@@ -308,12 +326,12 @@
     run = pl.pallas_call(
         kernel,
         out_shape=jax.ShapeDtypeStruct((256, C), f32),
-        in_specs=[pl.BlockSpec(memory_space=pl.ANY)] * 6,
+        in_specs=[pl.BlockSpec(memory_space=pl.ANY)] * 5 + [pl.BlockSpec(memory_space=pltpu.SMEM)],
         out_specs=pl.BlockSpec(memory_space=pltpu.VMEM),
         scratch_shapes=[
             V((64, 2, 2, 8, D), bf16), V((64, 2, 8, 128), f32), V((C, D), bf16), V((D, C), bf16), V((8, C), f32),
             V((RING, J, D), f32), V((RING, J, D), f32),
-            V((3 * M, C), bf16), V((3 * M, C), bf16), V((3, M, C), f32), V((3, M, C), f32),
+            V((3 * M, C), bf16), V((3 * M, C), bf16), V((3, C // 128, M, 128), f32), V((3, C // 128, M, 128), f32),
             V((8, D), f32), V((3, 2, 8, C), f32), V((2, 8, D), f32), V((4, 4, 4, 2, 2, C), f32),
             dma((6,)), dma, dma, dma((NB,)), dma((NB,)), dma((NB,)), dma((NB,)), dma((NB,)), dma((NB,)), dma, dma((4,)),
         ],
@@ -321,8 +339,7 @@
     )
 
     def local_run(x_init, w_in, w_out, mod_gamma, mod_beta, step_size):
-        hb = jnp.broadcast_to(step_size[:, None], (8, 128))
-        y = run(x_init.reshape(256, C), w_in, w_out, mod_gamma, mod_beta, hb)
+        y = run(x_init.reshape(256, C), w_in, w_out, mod_gamma, mod_beta, step_size)
         return y.reshape(x_init.shape)
 
     return jax.shard_map(local_run, mesh=mesh, in_specs=(P("data", None, None), P(None, None), P(None, None), P("time", None), P("time", None), P("time")), out_specs=P("data", None, None), check_vma=False)

time: 160 us -> 153 us (0.956)
  Pallas kernels: 157 us -> 151 us
    pallas_call x1, Pallas kernels: 157 us -> 151 us  [local_run(): y = run(x_init.reshape(256, C), w_in, w_out, mod_gamma, mod_beta, step_size)]
where the time goes in v3:
time: 153 us
  Pallas kernels  151 us (99%)
  local copies, waits for them, and re-layouts  2.09 us (1%)
    pallas_call x1, Pallas kernels, local_run(): y = run(x_init.reshape(256, C), w_in, w_out, mod_gamma, mod_beta, step_size)  151 us

profile of v3, /device:TPU:1, one launch (start us, length us, event | category | flops | bytes accessed | tf_op | source)
XLA Modules:
  0.0 152.6 jit_solution(7570331312353783289)
XLA Ops:
  0.0 150.5 %shard_map.64 = f32[256,768]{1,0:T(8,128)} custom-call(f32[256,768]{1,0:T(8,128)} %bitcast.3, bf16[768,3072]{1,0:T(8,128)(2,1)} %win_hbm.1, bf16[3072,768]{1,0:T(8,128)(2,1)} %wout_hbm.1, bf16[8,3072]{1,0:T(8,128)(2,1)} %gam_hbm.1, bf16[8,3072]{1,0:T(8,128)(2,1)} %bet_hbm.1, f32[8]{0:T(128)} %h_smem.1), custom_call_target="tpu_custom_call" | custom-call | tf_op jit(solution)/shard_map/pallas_call | solution.py:342
  150.5 2.1 %copy.8 = f32[4,64,768]{2,1,0:T(8,128)} copy(f32[4,64,768]{2,1,0:T(8,128)} %bitcast.2) | data formatting | bytes 1572864
